TPU v7x, 32 devices: a whole 2x2x4 slice. The times are simulated.
32 devices in a mesh: lat: 8 (over z, x), lev: 4 (over y, core).
Axes of the slice: x: 2, y: 2, z: 4, core: 2. Of those that a mesh axis runs over, the one named last changes fastest.
Arguments:
- grid: bfloat16 [640, 128, 4, 1280], P('lat', 'lev'), may hold values from -6 to 6
- legendre: bfloat16 [640, 640, 640], P('lat'), may hold values from -0.25 to 0.25
- vertical: bfloat16 [128, 128], P('lev'), may hold values from -0.5 to 0.5
- damping: bfloat16 [128], P('lev'), may hold values from 1 to 16
- lon_counts: int32 [640], replicated, may hold values from 160 to 1280
- wave_slots: int32 [640], replicated, may hold values from 0 to 639, as said below
Outputs:
- filtered_grid: bfloat16 [640, 128, 4, 1280], P('lat', 'lev')
Inputs may be any that keep to these rules, and one draw needn't show every extreme that they name: wave_slots is a permutation; slot g * 20 + r holds a wavenumber from r * 32 to (r + 1) * 32 - 1.
All inputs are finite; a program needn't handle non-finite values.
Results may differ from a plain program's by a relative error of at most 0.0074.
Values may be sent and summed in bfloat16 or wider, within the bound.
A program may use at most 512 MiB of HBM per device.

v0:
```python
import math
import jax
import jax.numpy as jnp
from jax import lax
from jax.sharding import PartitionSpec as P


def forward_build(wavenumbers, longitudes):
    points = jnp.arange(longitudes, dtype=jnp.int32)
    phase = (wavenumbers[:, None] * points[None, :] % longitudes).astype(jnp.float32) * (
        2.0 * math.pi / longitudes
    )
    scale = 1.0 / math.sqrt(longitudes)
    return jnp.stack([jnp.cos(phase) * scale, -jnp.sin(phase) * scale], axis=1).astype(jnp.bfloat16)


def inverse_build(wavenumbers, longitudes):
    points = jnp.arange(longitudes, dtype=jnp.int32)
    phase = (wavenumbers[:, None] * points[None, :] % longitudes).astype(jnp.float32) * (
        2.0 * math.pi / longitudes
    )
    scale = 1.0 / math.sqrt(longitudes)
    weight = jnp.where(wavenumbers == 0, 1.0, 2.0).astype(jnp.float32)[:, None]
    return jnp.stack(
        [jnp.cos(phase) * scale * weight, -jnp.sin(phase) * scale * weight], axis=1
    ).astype(jnp.bfloat16)


def damping_factor(degrees, damping):
    degree_values = jnp.arange(degrees).astype(jnp.float32)
    ratio = degree_values * (degree_values + 1.0) / float(degrees * (degrees - 1))
    return 1.0 / (1.0 + damping.astype(jnp.float32)[None, :] * (ratio * ratio)[:, None])


def legendre_forward(table, fourier, wavenumbers):
    degrees = table.shape[1]
    spectral = jnp.einsum("sna,srac->snrc", table, fourier, preferred_element_type=jnp.float32)
    live = (jnp.arange(degrees, dtype=jnp.int32)[None, :] >= wavenumbers[:, None]).astype(
        jnp.float32
    )
    return (spectral * live[:, :, None, None]).astype(jnp.bfloat16)


def legendre_inverse(table, mixed):
    banded = jnp.einsum("sna,snrc->srac", table, mixed, preferred_element_type=jnp.float32)
    return banded.astype(jnp.bfloat16)


def per_device(grid, legendre, vertical, damping, lon_counts, wave_slots):
    lat_rows, level_rows, fields, longitudes = grid.shape
    slot_count = wave_slots.shape[0]
    degrees = legendre.shape[1]
    forward_table = forward_build(wave_slots, longitudes)
    own_counts = lax.dynamic_slice_in_dim(lon_counts, lax.axis_index("lat") * lat_rows, lat_rows)
    fourier = jnp.einsum("mrx,alfx->mralf", forward_table, grid, preferred_element_type=jnp.float32)
    fourier = fourier.reshape(slot_count, 2, lat_rows, level_rows * fields)
    forward_kept = (2 * wave_slots[:, None] < own_counts[None, :]).astype(jnp.float32)
    fourier = (fourier * forward_kept[:, None, :, None]).astype(jnp.bfloat16)
    gathered = lax.all_to_all(fourier, "lat", split_axis=0, concat_axis=2, tiled=True)
    count = gathered.shape[0]
    own_waves = lax.dynamic_slice_in_dim(wave_slots, lax.axis_index("lat") * count, count)
    spectral = legendre_forward(legendre, gathered, own_waves)
    piece = lax.all_gather(spectral, "lev", axis=3, tiled=True)
    level_count = piece.shape[3] // fields
    block = piece.reshape(piece.shape[0], piece.shape[1], 2, level_count, fields)
    folded = jnp.einsum("snrkf,lk->snrlf", block, vertical, preferred_element_type=jnp.float32)
    own_part = spectral.reshape(count, degrees, 2, level_rows, fields).astype(jnp.float32)
    mixed = (own_part + folded) * damping_factor(degrees, damping)[None, :, None, :, None]
    mixed = mixed.astype(jnp.bfloat16).reshape(count, degrees, 2, level_rows * fields)
    banded = legendre_inverse(legendre, mixed)
    returned = lax.all_to_all(banded, "lat", split_axis=2, concat_axis=0, tiled=True)
    inverse_table = inverse_build(wave_slots, longitudes)
    back_kept = (2 * wave_slots[:, None] < own_counts[None, :]).astype(jnp.bfloat16)
    returned = returned * back_kept[:, None, :, None]
    filtered_grid = jnp.einsum(
        "mrac,mrx->acx", returned, inverse_table, preferred_element_type=jnp.float32
    )
    return filtered_grid.reshape(lat_rows, level_rows, fields, longitudes).astype(jnp.bfloat16)


def solution(mesh):
    return jax.shard_map(
        per_device,
        mesh=mesh,
        in_specs=(
            P("lat", "lev", None, None),
            P("lat", None, None),
            P("lev", None),
            P("lev"),
            P(),
            P(),
        ),
        out_specs=P("lat", "lev", None, None),
        check_vma=False,
    )
```

profile of v0, /device:TPU:0, one launch (start us, length us, event | category | flops | bytes accessed | tf_op | source)
XLA Modules:
  0.0 2570.0 jit_solution(2957762633101189925)
XLA Ops:
  6.5 0.0 copy-start
  6.5 0.7 broadcast_multiply_fusion
  7.2 0.7 select_multiply_fusion
  7.9 17.2 multiply_convert_fusion.3
  25.1 55.3 %fusion.9 = f32[640,2,80,32,4]{0,2,4,3,1:T(8,128)} fusion(bf16[80,32,4,1280]{3,2,1,0:T(4,128)(2,1)} %param.6, bf16[640,1,1280]{2,0,1:T(8,128)(2,1)S(1)} %get-tuple-element.9, bf16[640,1,1280]{2,0,1:T(8,128)(2,1)S(1)} %get-tuple-element.10), kind=kOutput, calls=%fused_computation.14 | convolution fusion | flops 33560985600 | bytes 81920000 | tf_op jit(solution)/shard_map/mrx,alfx->mralf/dot_general | solution.py:55
  80.4 58.4 %copy.27 = f32[640,2,80,128]{3,2,1,0:T(8,128)} copy(f32[640,2,80,128]{0,2,3,1:T(8,128)} %bitcast.69) | data formatting | bytes 104857600 | tf_op jit(solution)/shard_map/reshape | solution.py:56
  138.9 0.8 dynamic_slice.6
  139.6 0.8 compare_convert_fusion
  140.4 26.3 %multiply_convert_fusion.1 = bf16[640,2,80,128]{3,2,1,0:T(8,128)(2,1)} fusion(f32[640,2,80,128]{3,2,1,0:T(8,128)} %copy.27, f32[640,80]{1,0:T(8,128)S(1)} %get-tuple-element.8), kind=kLoop, calls=%fused_computation.11 | loop fusion | flops 26214400 | bytes 78848000 | tf_op jit(solution)/shard_map/convert_element_type | solution.py:58
  166.7 18.2 all-to-all-start
  184.9 0.0 all-gather.2.cloned.1.call-start
  185.0 0.8 dynamic_slice.7
  185.7 0.1 fusion.32
  185.8 565.9 %all-to-all-done = bf16[640,2,80,128]{3,2,1,0:T(8,128)(2,1)} async-done(((bf16[640,2,80,128]{3,2,1,0:T(8,128)(2,1)}), bf16[640,2,80,128]{3,2,1,0:T(8,128)(2,1)}, u32[]{:S(2)}, u32[]{:S(2)}) %all-to-all-start) | async-done | bytes 26214432 | tf_op jit(solution)/shard_map/all_to_all | solution.py:59
  751.8 21.8 copy.28
  773.6 42.9 %fusion.8 = bf16[80,640,2,128]{1,3,2,0:T(8,128)(2,1)} fusion(f32[80,640]{1,0:T(8,128)S(1)} %fusion.32, bf16[80,2,640,128]{3,2,1,0:T(8,128)(2,1)} %bitcast.71, bf16[80,640,640]{2,1,0:T(8,128)(2,1)} %param.7), kind=kOutput, calls=%fused_computation.12 | convolution fusion | flops 16803430400 | bytes 118169600 | tf_op jit(solution)/shard_map/sna,srac->snrc/dot_general | solution.py:37
  816.5 0.0 copy-start.5
  816.5 0.0 all-gather.2.cloned.1.call-update
  816.6 0.6 copy-done.5
  817.2 0.1 add_divide_fusion
  817.3 50.3 %reshape.290 = f32[80,640,2,32,4]{1,4,3,2,0:T(4,128)} reshape(bf16[80,640,2,128]{1,3,2,0:T(8,128)(2,1)} %fusion.8) | data formatting | bytes 78643200 | tf_op jit(solution)/shard_map/convert_element_type | solution.py:67
  867.6 557.3 %all-gather.2.cloned.1.call-done = bf16[80,640,2,512]{1,3,2,0:T(8,128)(2,1)} async-done(((bf16[80,640,2,128]{1,3,2,0:T(8,128)(2,1)}), bf16[80,640,2,512]{1,3,2,0:T(8,128)(2,1)}) %all-gather.2.cloned.1.call-update) | async-done | bytes 104857616 | tf_op jit(solution)/shard_map/all_gather | solution.py:63
  1424.9 168.4 %reshape.288 = bf16[80,640,2,128,4]{1,4,3,2,0:T(4,128)(2,1)} reshape(bf16[80,640,2,512]{1,3,2,0:T(8,128)(2,1)} %all-gather.2.cloned.1.call-done) | data formatting | bytes 209715200 | tf_op jit(solution)/shard_map/reshape | solution.py:65
  1593.3 0.0 copy-done
  1593.3 64.9 %fusion.7 = bf16[80,640,2,32,4]{1,3,4,2,0:T(8,128)(2,1)} fusion(f32[80,640,2,32,4]{1,4,3,2,0:T(4,128)} %reshape.290, f32[640,32]{0,1:T(8,128)S(1)} %add_divide_fusion, bf16[80,640,2,128,4]{1,4,3,2,0:T(4,128)(2,1)} %reshape.288, bf16[32,128]{1,0:T(8,128)(2,1)S(1)} %copy-done), kind=kOutput, calls=%fused_computation.9 | convolution fusion | flops 3394764800 | bytes 183590912 | tf_op jit(solution)/shard_map/snrkf,lk->snrlf/dot_general | solution.py:66
  1658.2 18.6 copy.32
  1676.8 54.9 %convert_bitcast_fusion = bf16[80,2,640,128]{2,3,1,0:T(8,128)(2,1)} fusion(bf16[80,640,640]{2,1,0:T(8,128)(2,1)} %param.7, bf16[80,640,2,128]{1,0,3,2:T(8,128)(2,1)} %bitcast.72), kind=kOutput, calls=%fused_computation.19 | convolution fusion | flops 16790323200 | bytes 117964800 | tf_op jit(solution)/shard_map/sna,snrc->srac/dot_general | solution.py:45
  1731.7 64.2 %copy.34 = bf16[80,2,640,128]{3,1,0,2:T(2,128)(2,1)} copy(bf16[80,2,640,128]{2,3,1,0:T(8,128)(2,1)} %convert_bitcast_fusion) | data formatting | bytes 52428800 | tf_op jit(solution)/shard_map/convert_element_type | solution.py:46
  1795.9 570.9 %all_to_all.36 = bf16[80,2,640,128]{3,1,0,2:T(2,128)(2,1)S(1)} all-to-all(bf16[80,2,640,128]{3,1,0,2:T(2,128)(2,1)} %copy.34), channel_id=1, replica_groups=mesh['lat'=8,'lev'=4] {'lat'}, dimensions={2} | all-to-all | bytes 52428800 | tf_op jit(solution)/shard_map/all_to_all | solution.py:71
  2366.9 12.7 copy.35
  2379.6 0.0 copy-start.4
  2379.6 21.3 copy.36
  2400.8 0.0 copy-done.4
  2400.8 18.0 bitcast_multiply_fusion
  2418.8 0.0 copy-start.2
  2418.8 0.0 copy-start.3
  2418.8 42.8 %copy.37 = bf16[80,128,640,2]{2,0,3,1:T(8,128)(2,1)} copy(bf16[80,128,640,2]{1,0,3,2:T(8,128)(2,1)} %bitcast.67) | data formatting | bytes 52428800 | tf_op jit(solution)/shard_map/mrac,mrx->acx/dot_general | solution.py:75
  2461.6 0.0 copy-done.2
  2461.6 0.0 copy-done.3
  2461.6 0.0 copy-start.1
  2461.7 71.1 %bitcast_convert_fusion = bf16[80,32,4,1280]{3,1,2,0:T(8,128)(2,1)} fusion(bf16[80,32,4,640,2]{3,0,4,2,1:T(8,128)(2,1)} %bitcast.70, bf16[640,1,1280]{2,0,1:T(8,128)(2,1)S(1)} %copy-done.3, bf16[640,1,1280]{2,0,1:T(8,128)(2,1)S(1)} %copy-done.2), kind=kOutput, calls=%fused_computation.6 | convolution fusion | flops 33569177600 | bytes 55705600 | tf_op jit(solution)/shard_map/mrac,mrx->acx/dot_general | solution.py:75
  2532.8 29.9 %copy.39 = bf16[80,32,4,1280]{3,2,1,0:T(4,128)(2,1)} copy(bf16[80,32,4,1280]{3,1,2,0:T(8,128)(2,1)} %bitcast_convert_fusion) | data formatting | bytes 52428800 | tf_op jit(solution)/shard_map/convert_element_type | solution.py:78
  2562.7 0.0 copy-done.1
  (2 shorter events, 0.0 us)
Async XLA Ops:
  6.5 1586.7 %copy-start = (bf16[32,128]{1,0:T(8,128)(2,1)S(1)}, bf16[32,128]{1,0:T(8,128)(2,1)}, u32[]{:S(2)}) copy-start(bf16[32,128]{1,0:T(8,128)(2,1)} %param.8) | copy-start | bytes 24580
  166.7 585.0 %all-to-all-start = ((bf16[640,2,80,128]{3,2,1,0:T(8,128)(2,1)}), bf16[640,2,80,128]{3,2,1,0:T(8,128)(2,1)}, u32[]{:S(2)}, u32[]{:S(2)}) async-start(bf16[640,2,80,128]{3,2,1,0:T(8,128)(2,1)} %multiply_convert_fusion.1), calls=%async_computation | async-start | bytes 52428800 | tf_op jit(solution)/shard_map/all_to_all | solution.py:59
  184.9 1240.0 %all-gather.2.cloned.1.call-start = ((), (), s32[]{:S(2)}) async-start(), calls=%async_computation.2 | async-start | bytes 131072000 | tf_op jit(solution)/shard_map/all_gather | solution.py:63
  816.5 0.7 copy-start.5
  2379.6 21.3 copy-start.4
  2418.8 42.8 %copy-start.2 = (bf16[640,1,1280]{2,0,1:T(8,128)(2,1)S(1)}, bf16[640,1,1280]{2,0,1:T(8,128)(2,1)}, u32[]{:S(2)}) copy-start(bf16[640,1,1280]{2,0,1:T(8,128)(2,1)} %get-tuple-element.5) | copy-start | bytes 4915204
  2418.8 42.9 %copy-start.3 = (bf16[640,1,1280]{2,0,1:T(8,128)(2,1)S(1)}, bf16[640,1,1280]{2,0,1:T(8,128)(2,1)}, u32[]{:S(2)}) copy-start(bf16[640,1,1280]{2,0,1:T(8,128)(2,1)} %get-tuple-element.6) | copy-start | bytes 4915204
  2461.6 101.1 %copy-start.1 = (bf16[32,128]{1,0:T(8,128)(2,1)S(1)}, bf16[32,128]{1,0:T(8,128)(2,1)}, u32[]{:S(2)}) copy-start(bf16[32,128]{1,0:T(8,128)(2,1)} %param.8) | copy-start | bytes 24580
Sparse Core Ops, SparseCore 0:
  816.7 608.1 all-gather.1
where the time goes:
time: 2590 us; the launch traced here: 2570 us
  waiting for transfers between devices  1120 us (43%)
  blocking collectives  571 us (22%)
  local copies, waits for them, and re-layouts  491 us (19%)
  matrix products  289 us (11%)
  other arithmetic  63.8 us (2%)
    all_to_all x1, blocking collectives, per_device(): lax.all_to_all(banded, 'lat', split_axis=2, concat_axis=0, tiled=True)  571 us
    all_to_all x1, waiting for transfers between devices, per_device(): lax.all_to_all(fourier, 'lat', split_axis=0, concat_axis=2, tiled=True)  566 us
    all_gather x1, waiting for transfers between devices, per_device(): piece = lax.all_gather(spectral, 'lev', axis=3, tiled=True)  557 us
    reshape x1, local copies, waits for them, and re-layouts, per_device(): piece.reshape(piece.shape[0], piece.shape[1], 2, level_count, fields)  168 us
    dot_general x1, matrix products, per_device(): jnp.einsum('mrac,mrx->acx', returned, inverse_table, preferred_element_ty...  71.1 us
    dot_general x1, matrix products, per_device(): jnp.einsum('snrkf,lk->snrlf', block, vertical, preferred_element_type=jnp...  64.9 us
    convert_element_type x1, local copies, waits for them, and re-layouts, legendre_inverse(): return banded.astype(jnp.bfloat16)  64.2 us
    reshape x1, local copies, waits for them, and re-layouts, per_device(): fourier = fourier.reshape(slot_count, 2, lat_rows, level_rows * fields)  58.4 us
  transfers between devices with their start and end apart: 2, of which 2 were waited for; matrix products, arithmetic and copies ran while one was open for 2% of the time, Pallas kernels for 0%

commit v1 on v0

--- a/solution.py
+++ b/solution.py
@@ -68,7 +68,10 @@
     mixed = (own_part + folded) * damping_factor(degrees, damping)[None, :, None, :, None]
     mixed = mixed.astype(jnp.bfloat16).reshape(count, degrees, 2, level_rows * fields)
     banded = legendre_inverse(legendre, mixed)
-    returned = lax.all_to_all(banded, "lat", split_axis=2, concat_axis=0, tiled=True)
+    returned = jnp.concatenate(
+        lax.all_to_all(jnp.stack(jnp.split(banded, lax.axis_size("lat"), axis=2)), "lat", 0, 0),
+        axis=0,
+    )
     inverse_table = inverse_build(wave_slots, longitudes)
     back_kept = (2 * wave_slots[:, None] < own_counts[None, :]).astype(jnp.bfloat16)
     returned = returned * back_kept[:, None, :, None]

time: 2590 us -> 2590 us (level)
    convert_element_type x1 -> x0, local copies, waits for them, and re-layouts: 64.2 us -> none  [legendre_inverse(): return banded.astype(jnp.bfloat16)]
    unnamed x12 -> x19, local copies, waits for them, and re-layouts: 0.65 us -> 53.2 us
    another operation x0 -> x2, local copies, waits for them, and re-layouts: none -> 49.6 us  [per_device(): jnp.stack(jnp.split(banded, lax.axis_size('lat'), axis=2))]
    all_to_all x2 -> x0, local copies, waits for them, and re-layouts: 34 us -> none  [per_device(): lax.all_to_all(banded, 'lat', split_axis=2, concat_axis=0, tiled=True)]
where the time goes in v1:
time: 2590 us; the launch traced here: 2570 us
  waiting for transfers between devices  1120 us (43%)
  blocking collectives  575 us (22%)
  local copies, waits for them, and re-layouts  495 us (19%)
  matrix products  289 us (11%)
  other arithmetic  63.8 us (2%)
    all_to_all x1, blocking collectives, per_device(): lax.all_to_all(jnp.stack(jnp.split(banded, lax.axis_size('lat'), axis=2))...  575 us
    all_to_all x1, waiting for transfers between devices, per_device(): lax.all_to_all(fourier, 'lat', split_axis=0, concat_axis=2, tiled=True)  566 us
    all_gather x1, waiting for transfers between devices, per_device(): piece = lax.all_gather(spectral, 'lev', axis=3, tiled=True)  557 us
    reshape x1, local copies, waits for them, and re-layouts, per_device(): piece.reshape(piece.shape[0], piece.shape[1], 2, level_count, fields)  168 us
    dot_general x1, matrix products, per_device(): jnp.einsum('mrac,mrx->acx', returned, inverse_table, preferred_element_ty...  71 us
    dot_general x1, matrix products, per_device(): jnp.einsum('snrkf,lk->snrlf', block, vertical, preferred_element_type=jnp...  64.9 us
    reshape x1, local copies, waits for them, and re-layouts, per_device(): fourier = fourier.reshape(slot_count, 2, lat_rows, level_rows * fields)  58.4 us
    dot_general x1, matrix products, per_device(): jnp.einsum('mrx,alfx->mralf', forward_table, grid, preferred_element_type...  55.3 us
  transfers between devices with their start and end apart: 2, of which 2 were waited for; matrix products, arithmetic and copies ran while one was open for 2% of the time, Pallas kernels for 0%

profile of v1, /device:TPU:0, one launch (start us, length us, event | category | flops | bytes accessed | tf_op | source)
XLA Modules:
  0.0 2567.2 jit_solution(14363074901066134418)
XLA Ops:
  6.5 0.0 copy-start
  6.5 0.7 broadcast_multiply_fusion
  7.2 0.7 select_multiply_fusion
  7.9 17.2 multiply_convert_fusion.3
  25.1 55.3 %fusion.9 = f32[640,2,80,32,4]{0,2,4,3,1:T(8,128)} fusion(bf16[80,32,4,1280]{3,2,1,0:T(4,128)(2,1)} %param.6, bf16[640,1,1280]{2,0,1:T(8,128)(2,1)S(1)} %get-tuple-element.9, bf16[640,1,1280]{2,0,1:T(8,128)(2,1)S(1)} %get-tuple-element.10), kind=kOutput, calls=%fused_computation.14 | convolution fusion | flops 33560985600 | bytes 81920000 | tf_op jit(solution)/shard_map/mrx,alfx->mralf/dot_general | solution.py:55
  80.4 58.4 %copy.39 = f32[640,2,80,128]{3,2,1,0:T(8,128)} copy(f32[640,2,80,128]{0,2,3,1:T(8,128)} %bitcast.97) | data formatting | bytes 104857600 | tf_op jit(solution)/shard_map/reshape | solution.py:56
  138.9 0.8 dynamic_slice.6
  139.6 0.8 compare_convert_fusion
  140.4 26.3 %multiply_convert_fusion.1 = bf16[640,2,80,128]{3,2,1,0:T(8,128)(2,1)} fusion(f32[640,2,80,128]{3,2,1,0:T(8,128)} %copy.39, f32[640,80]{1,0:T(8,128)S(1)} %get-tuple-element.8), kind=kLoop, calls=%fused_computation.11 | loop fusion | flops 26214400 | bytes 78848000 | tf_op jit(solution)/shard_map/convert_element_type | solution.py:58
  166.7 7.3 all-to-all-start
  174.0 0.0 all-gather.2.cloned.1.call-start
  174.0 0.8 dynamic_slice.7
  174.8 0.1 fusion.40
  174.9 565.8 %all-to-all-done = bf16[640,2,80,128]{3,2,1,0:T(8,128)(2,1)} async-done(((bf16[640,2,80,128]{3,2,1,0:T(8,128)(2,1)}), bf16[640,2,80,128]{3,2,1,0:T(8,128)(2,1)}, u32[]{:S(2)}, u32[]{:S(2)}) %all-to-all-start) | async-done | bytes 26214432 | tf_op jit(solution)/shard_map/all_to_all | solution.py:59
  740.7 21.8 copy.40
  762.5 42.9 %fusion.8 = bf16[80,640,2,128]{1,3,2,0:T(8,128)(2,1)} fusion(f32[80,640]{1,0:T(8,128)S(1)} %fusion.40, bf16[80,2,640,128]{3,2,1,0:T(8,128)(2,1)} %bitcast.99, bf16[80,640,640]{2,1,0:T(8,128)(2,1)} %param.7), kind=kOutput, calls=%fused_computation.12 | convolution fusion | flops 16803430400 | bytes 118169600 | tf_op jit(solution)/shard_map/sna,srac->snrc/dot_general | solution.py:37
  805.4 0.0 copy-start.5
  805.4 0.0 all-gather.2.cloned.1.call-update
  805.5 0.6 copy-done.5
  806.1 0.1 add_divide_fusion
  806.2 50.3 %reshape.294 = f32[80,640,2,32,4]{1,4,3,2,0:T(4,128)} reshape(bf16[80,640,2,128]{1,3,2,0:T(8,128)(2,1)} %fusion.8) | data formatting | bytes 78643200 | tf_op jit(solution)/shard_map/convert_element_type | solution.py:67
  856.5 557.1 %all-gather.2.cloned.1.call-done = bf16[80,640,2,512]{1,3,2,0:T(8,128)(2,1)} async-done(((bf16[80,640,2,128]{1,3,2,0:T(8,128)(2,1)}), bf16[80,640,2,512]{1,3,2,0:T(8,128)(2,1)}) %all-gather.2.cloned.1.call-update) | async-done | bytes 104857616 | tf_op jit(solution)/shard_map/all_gather | solution.py:63
  1413.6 168.4 %reshape.291 = bf16[80,640,2,128,4]{1,4,3,2,0:T(4,128)(2,1)} reshape(bf16[80,640,2,512]{1,3,2,0:T(8,128)(2,1)} %all-gather.2.cloned.1.call-done) | data formatting | bytes 209715200 | tf_op jit(solution)/shard_map/reshape | solution.py:65
  1581.9 0.0 copy-done
  1581.9 64.9 %fusion.7 = bf16[80,640,2,32,4]{1,3,4,2,0:T(8,128)(2,1)} fusion(f32[80,640,2,32,4]{1,4,3,2,0:T(4,128)} %reshape.294, f32[640,32]{0,1:T(8,128)S(1)} %add_divide_fusion, bf16[80,640,2,128,4]{1,4,3,2,0:T(4,128)(2,1)} %reshape.291, bf16[32,128]{1,0:T(8,128)(2,1)S(1)} %copy-done), kind=kOutput, calls=%fused_computation.9 | convolution fusion | flops 3394764800 | bytes 183590912 | tf_op jit(solution)/shard_map/snrkf,lk->snrlf/dot_general | solution.py:66
  1646.9 18.6 copy.44
  1665.5 55.1 %convert_bitcast_fusion = bf16[80,2,640,128]{2,3,1,0:T(8,128)(2,1)} fusion(bf16[80,640,640]{2,1,0:T(8,128)(2,1)} %param.7, bf16[80,640,2,128]{1,0,3,2:T(8,128)(2,1)} %bitcast.100), kind=kOutput, calls=%fused_computation.19 | convolution fusion | flops 16790323200 | bytes 117964800 | tf_op jit(solution)/shard_map/sna,snrc->srac/dot_general | solution.py:45
  1720.6 6.9 fusion.29
  1727.5 8.3 fusion.28
  1735.8 6.4 fusion.27
  1742.2 8.2 fusion.26
  1750.4 8.2 fusion.25
  1758.6 6.4 fusion.24
  1765.0 8.1 fusion.23
  1773.2 6.5 fusion.22
  1779.7 43.1 %copy.46 = bf16[8,80,2,80,128]{4,3,2,1,0:T(8,128)(2,1)} copy(bf16[8,80,2,80,128]{3,4,2,1,0:T(8,128)(2,1)} %fusion.22) | data formatting | bytes 52428800 | tf_op jit(solution)/shard_map/stack | solution.py:72
  1822.8 0.0 copy-start.4
  1822.8 575.5 %all_to_all.23 = bf16[8,80,2,80,128]{4,3,2,1,0:T(8,128)(2,1)} all-to-all(bf16[8,80,2,80,128]{4,3,2,1,0:T(8,128)(2,1)} %copy.46), channel_id=1, replica_groups=mesh['lat'=8,'lev'=4] {'lat'}, dimensions={0} | all-to-all | bytes 52428800 | tf_op jit(solution)/shard_map/all_to_all | solution.py:72
  2398.3 0.0 copy-done.4
  2398.3 18.0 bitcast_multiply_fusion
  2416.2 0.0 copy-start.3
  2416.2 42.8 %copy.47 = bf16[80,128,640,2]{2,0,3,1:T(8,128)(2,1)} copy(bf16[80,128,640,2]{1,0,3,2:T(8,128)(2,1)} %bitcast.96) | data formatting | bytes 52428800 | tf_op jit(solution)/shard_map/mrac,mrx->acx/dot_general | solution.py:78
  2459.1 0.0 copy-done.2
  2459.1 0.0 copy-done.3
  2459.1 0.0 copy-start.1
  2459.1 71.0 %bitcast_convert_fusion = bf16[80,32,4,1280]{3,1,2,0:T(8,128)(2,1)} fusion(bf16[80,32,4,640,2]{3,0,4,2,1:T(8,128)(2,1)} %bitcast.98, bf16[640,1,1280]{2,0,1:T(8,128)(2,1)S(1)} %copy-done.3, bf16[640,1,1280]{2,0,1:T(8,128)(2,1)S(1)} %copy-done.2), kind=kOutput, calls=%fused_computation.6 | convolution fusion | flops 33569177600 | bytes 55705600 | tf_op jit(solution)/shard_map/mrac,mrx->acx/dot_general | solution.py:78
  2530.1 29.9 %copy.49 = bf16[80,32,4,1280]{3,2,1,0:T(4,128)(2,1)} copy(bf16[80,32,4,1280]{3,1,2,0:T(8,128)(2,1)} %bitcast_convert_fusion) | data formatting | bytes 52428800 | tf_op jit(solution)/shard_map/convert_element_type | solution.py:81
  2560.0 0.0 copy-done.1
  (3 shorter events, 0.0 us)
Async XLA Ops:
  6.5 1575.4 %copy-start = (bf16[32,128]{1,0:T(8,128)(2,1)S(1)}, bf16[32,128]{1,0:T(8,128)(2,1)}, u32[]{:S(2)}) copy-start(bf16[32,128]{1,0:T(8,128)(2,1)} %param.8) | copy-start | bytes 24580
  166.7 574.0 %all-to-all-start = ((bf16[640,2,80,128]{3,2,1,0:T(8,128)(2,1)}), bf16[640,2,80,128]{3,2,1,0:T(8,128)(2,1)}, u32[]{:S(2)}, u32[]{:S(2)}) async-start(bf16[640,2,80,128]{3,2,1,0:T(8,128)(2,1)} %multiply_convert_fusion.1), calls=%async_computation | async-start | bytes 52428800 | tf_op jit(solution)/shard_map/all_to_all | solution.py:59
  174.0 1239.6 %all-gather.2.cloned.1.call-start = ((), (), s32[]{:S(2)}) async-start(), calls=%async_computation.2 | async-start | bytes 131072000 | tf_op jit(solution)/shard_map/all_gather | solution.py:63
  805.4 0.7 copy-start.5
  1822.8 575.5 %copy-start.4 = (bf16[640,80]{1,0:T(8,128)(2,1)S(1)}, bf16[640,80]{1,0:T(8,128)(2,1)}, u32[]{:S(2)}) copy-start(bf16[640,80]{1,0:T(8,128)(2,1)} %get-tuple-element.7) | copy-start | bytes 307204
  2416.2 42.8 %copy-start.2 = (bf16[640,1,1280]{2,0,1:T(8,128)(2,1)S(1)}, bf16[640,1,1280]{2,0,1:T(8,128)(2,1)}, u32[]{:S(2)}) copy-start(bf16[640,1,1280]{2,0,1:T(8,128)(2,1)} %get-tuple-element.5) | copy-start | bytes 4915204
  2416.2 42.9 %copy-start.3 = (bf16[640,1,1280]{2,0,1:T(8,128)(2,1)S(1)}, bf16[640,1,1280]{2,0,1:T(8,128)(2,1)}, u32[]{:S(2)}) copy-start(bf16[640,1,1280]{2,0,1:T(8,128)(2,1)} %get-tuple-element.6) | copy-start | bytes 4915204
  2459.1 100.9 %copy-start.1 = (bf16[32,128]{1,0:T(8,128)(2,1)S(1)}, bf16[32,128]{1,0:T(8,128)(2,1)}, u32[]{:S(2)}) copy-start(bf16[32,128]{1,0:T(8,128)(2,1)} %param.8) | copy-start | bytes 24580
Sparse Core Ops, SparseCore 0:
  805.6 607.9 all-gather.1
